TPU v7x, 8 devices: a whole 2x2x1 slice. The times are simulated.
8 devices in a mesh: dp: 1 (over z), col: 2 (over y), row: 4 (over x, core).
Axes of the slice: x: 2, y: 2, z: 1, core: 2. Of those that a mesh axis runs over, the one named last changes fastest.
Arguments:
- x_in: bfloat16 [2, 4096, 1024], P(None, ('dp', 'row'), 'col')
- ln_gamma: float32 [1024], P('col')
- w_in: bfloat16 [1024, 4096], P('row', 'col')
- w_out: bfloat16 [4096, 1024], P('row', 'col')
Outputs:
- output: bfloat16 [2, 4096, 1024], P(None, ('dp', 'row'), 'col')
All inputs are finite; a program needn't handle non-finite values.
Results may differ from a plain program's by a relative error of at most 0.001.
Values are sent between devices in bfloat16 or wider.
A program may use at most 1 GiB of HBM per device.

v0:
```python
import jax
import jax.numpy as jnp
from jax import lax
from jax.experimental import pallas as pl
from jax.experimental.pallas import tpu as pltpu
from jax.sharding import PartitionSpec as P

LN_EPS = 1e-5
MESH = pl.DeviceIdType.MESH
PC = 256
SQRT_2_OVER_PI = 0.7978845608028654
X_ROWS = ((0, 512), (512, 512), (1024, 512), (1536, 320), (1856, 192))

A_ICI, A_D2D, B_Y, B_X, B_D2D, X_Y, G_Y = 0, 4, 8, 24, 32, 40, 45
N_RECV = 46
S_W1, S_W2, S_X, S_G = 0, 1, 2, 3


def gelu(u):
    inner = u * (SQRT_2_OVER_PI + (SQRT_2_OVER_PI * 0.044715) * (u * u))
    return ((0.5 * u) * (1.0 + jnp.tanh(inner))).astype(jnp.bfloat16)


def kernel(x_hbm, g_hbm, w1_hbm, w2_hbm, ys, xs, w1s, w2s, zs, acc, gs, load_sem, send_sem, recv_sem):
    rows1 = w1_hbm.shape[0]
    tokens, d_model = zs.shape
    half_d = d_model // 2

    col = lax.axis_index("col")
    row = lax.axis_index("row")
    core = row % 2
    row_p = row + 1 - 2 * core
    row_x = (row + 2) % 4
    row_xp = (row_p + 2) % 4
    other = 1 - col
    partner, x_nbr, y_nbr = {"row": row_p}, {"row": row_x}, {"col": other}

    def w1p(half, e, r, n=1):
        return w1s.at[pl.ds(half * 8 + e, n), pl.ds(pl.multiple_of(r * rows1, rows1), rows1)]

    def w2p(r, j):
        return w2s.at[(r // 2) * 8 + 2 * j + r % 2]

    def send(ref, dev, s_sem, r_sem):
        pltpu.make_async_remote_copy(
            src_ref=ref, dst_ref=ref, send_sem=send_sem.at[s_sem], recv_sem=recv_sem.at[r_sem],
            device_id=dev, device_id_type=MESH).start()

    def wait(ref, sem):
        pltpu.make_async_copy(ref, ref, sem).wait()

    def load_w(s):
        for e in (2 * s, 2 * s + 1):
            cols = pl.ds((e % 2) * (4 * PC) + (e // 2) * PC, PC)
            dst = w1s.at[col * 8 + e, pl.ds(pl.multiple_of(row * rows1, rows1), rows1)]
            pltpu.make_async_copy(w1_hbm.at[:, cols], dst, load_sem.at[s]).start()
        pltpu.make_async_copy(w2_hbm.at[pl.ds(s * PC, PC)], w2p(row, s), load_sem.at[s]).start()

    def x_part(h, i):
        r0, n = X_ROWS[i]
        return xs.at[h, pl.ds(r0, n)]

    def load_x(i):
        r0, n = X_ROWS[i]
        pltpu.make_async_copy(x_hbm.at[pl.ds(r0, n)], x_part(col, i), load_sem.at[4 + i]).start()

    pltpu.make_async_copy(g_hbm, gs.at[col], load_sem.at[9]).start()
    for s in range(4):
        load_w(s)
        load_x(s)
    load_x(4)

    barrier = pltpu.get_barrier_semaphore()
    for dev in (partner, x_nbr, y_nbr):
        pl.semaphore_signal(barrier, inc=1, device_id=dev, device_id_type=MESH)
    pl.semaphore_wait(barrier, 3)

    def send_x(i):
        wait(x_part(col, i), load_sem.at[4 + i])
        send(x_part(col, i), y_nbr, S_X, X_Y + i)

    def issue(s):
        wait(w1s.at[0], load_sem.at[s])
        w1, w2 = w1p(col, 2 * s, row, 2), w2p(row, s)
        send(w1, x_nbr, S_W1, A_ICI + s)
        send(w2, x_nbr, S_W2, A_ICI + s)
        send(w1, partner, S_W1, A_D2D + s)
        send(w2, partner, S_W2, A_D2D + s)
        send_x(s)

    def relay_a(s):
        wait(w1s.at[0], recv_sem.at[A_ICI + s])
        send(w1p(col, 2 * s, row_x, 2), partner, S_W1, A_D2D + s)
        send(w2p(row_x, s), partner, S_W2, A_D2D + s)

    def half_piece(half, e, h):
        return w1s.at[half * 8 + e, pl.ds(pl.multiple_of(row * rows1 + h * (rows1 // 2), rows1 // 2), rows1 // 2)]

    def relay_by(e, h):
        part = half_piece(other, e, h)
        wait(part, recv_sem.at[B_Y + 2 * e + h])
        send(part, x_nbr, S_W1, B_X + e)
        send(part, partner, S_W1, B_D2D + e)

    def relay_bx(e):
        wait(w1p(other, e, row_x), recv_sem.at[B_X + e])
        send(w1p(other, e, row_x), partner, S_W1, B_D2D + e)

    def layer_norm(i):
        r0, n = X_ROWS[i]
        rb = 64
        wait(x_part(other, i), recv_sem.at[X_Y + i])

        def step(t, _):
            rows = pl.ds(pl.multiple_of(r0 + t * rb, rb), rb)
            parts = [xs[h, rows, :].astype(jnp.float32) for h in range(2)]
            mean = sum(jnp.sum(v, axis=-1, keepdims=True) for v in parts) / d_model
            var = sum(jnp.sum(v * v, axis=-1, keepdims=True) for v in parts) / d_model - mean * mean
            inv = lax.rsqrt(var + LN_EPS)
            for h in range(2):
                zs[rows, h * half_d:(h + 1) * half_d] = ((parts[h] - mean) * inv * gs[h]).astype(jnp.bfloat16)
            acc[rows, :] = xs[col, rows, :].astype(jnp.float32)
            return 0

        lax.fori_loop(0, n // rb, step, 0, unroll=n <= 192)

    held = []

    def finish():
        if held:
            r0, n, ps, hs, store = held.pop()
            rows = pl.ds(r0, n)
            out = None
            for p, h in zip(ps, hs):
                term = jnp.dot(h, w2s[p], preferred_element_type=jnp.float32)
                out = term if out is None else out + term
            if store is None:
                acc[rows, :] += out
            else:
                store(rows, acc[rows, :] + out)

    def unit(r0, n, ps, store=None):
        z = zs[pl.ds(r0, n), :]
        hs = [gelu(jnp.dot(z, w1s[p], preferred_element_type=jnp.float32)) for p in ps]
        finish()
        held.append((r0, n, ps, hs, store))

    def pieces(half, lo, hi):
        return [half * 8 + e for e in range(lo, hi)]

    with jax.named_scope("issue"):
        wait(gs.at[col], load_sem.at[9])
        send(gs.at[col], y_nbr, S_G, G_Y)
        issue(0)
        issue(1)
        wait(gs.at[other], recv_sem.at[G_Y])
    for s in range(3):
        with jax.named_scope(f"a_wait_x{s}"):
            if s < 2:
                issue(s + 2)
            if s == 1:
                for e in range(8):
                    for h in range(2):
                        send(half_piece(col, e, h), y_nbr, S_W1, B_Y + 2 * e + h)
                send_x(4)
            relay_a(s)
        with jax.named_scope(f"a_norm{s}"):
            layer_norm(s)
        with jax.named_scope(f"a_wait_d{s}"):
            wait(w1s.at[pl.ds(0, 2)], recv_sem.at[A_D2D + s])
        with jax.named_scope(f"a_tiles{s}"):
            def a_tile(t, _):
                q = t // (s + 1)
                g, j = t - q * (t - s), s - q * (t - s)
                p = col * 8 + 2 * j
                for k in (0, 256):
                    unit(pl.multiple_of(g * 512 + k, 256), 256, (p, p + 1))
                finish()
                return 0

            lax.fori_loop(0, 2 * s + 1, a_tile, 0)

    early = X_ROWS[4][0]
    third = early // 3
    with jax.named_scope("a_norm3"):
        layer_norm(3)
    quarter = early // 4

    def first(e):
        with jax.named_scope(f"first{e}"):
            unit(*X_ROWS[3], pieces(col, 2 * e, 2 * e + 2))

    def a_unit(q):
        unit(q * quarter, quarter, pieces(col, 6, 8))

    def b_unit(e, q):
        unit(q * quarter, quarter, pieces(other, e, e + 1))

    def by(e, h):
        with jax.named_scope(f"by{e}{h}"):
            relay_by(e, h)

    def bx(e):
        with jax.named_scope(f"bx{e}"):
            relay_bx(e)

    def b_arrived(e):
        with jax.named_scope(f"bd{e}"):
            wait(w2s.at[0], recv_sem.at[B_D2D + e])

    first(0)
    by(0, 0)
    first(1)
    first(2)
    by(0, 1)
    with jax.named_scope("a3"):
        relay_a(3)
    by(1, 0)
    with jax.named_scope("ad3"):
        wait(w1s.at[pl.ds(0, 2)], recv_sem.at[A_D2D + 3])
    a_unit(0)
    by(1, 1)
    a_unit(1)
    a_unit(2)
    bx(0)
    by(2, 0)
    a_unit(3)
    for e in range(5):
        by(e + 2, 1)
        b_arrived(e)
        b_unit(e, 0)
        b_unit(e, 1)
        bx(e + 1)
        by(e + 3, 0)
        b_unit(e, 2)
        b_unit(e, 3)
    by(7, 1)
    b_arrived(5)
    b_unit(5, 0)
    b_unit(5, 1)
    bx(6)
    b_unit(5, 2)
    b_unit(5, 3)
    b_arrived(6)
    for q in range(4):
        b_unit(6, q)
    finish()
    bx(7)
    with jax.named_scope("c_norm"):
        layer_norm(4)
    with jax.named_scope("c_tiles"):
        last = pieces(col, 0, 8) + pieces(other, 0, 7)
        unit(early, tokens - early, last[:8])
        unit(early, tokens - early, last[8:])
        finish()
    b_arrived(7)
    with jax.named_scope("d_tile"):
        def write(rows, value):
            ys[rows, :] = value.astype(jnp.bfloat16)

        for q in range(4):
            unit(q * (tokens // 4), tokens // 4, pieces(other, 7, 8), write)
        finish()

    with jax.named_scope("sent"):
        wait(w1s.at[pl.ds(0, 14)], send_sem.at[S_W1])
        wait(w2s.at[pl.ds(0, 12)], send_sem.at[S_W2])
        wait(xs.at[0], send_sem.at[S_X])
        wait(gs.at[0], send_sem.at[S_G])


def solution(mesh):
    act_spec = P(None, ("dp", "row"), "col")

    def per_device(x_blk, gamma_blk, w_in_blk, w_out_blk):
        feats = x_blk.shape[2]
        tokens = x_blk.shape[0] * x_blk.shape[1]
        d_model = 2 * feats
        n_pieces = 2 * w_in_blk.shape[1] // PC
        ins = (x_blk.reshape(tokens, feats), gamma_blk.reshape(1, feats), w_in_blk, w_out_blk)
        y = pl.pallas_call(
            kernel,
            name="mlp",
            out_shape=jax.ShapeDtypeStruct((tokens, feats), jnp.bfloat16),
            in_specs=[pl.BlockSpec(memory_space=pltpu.HBM)] * 4,
            out_specs=pl.BlockSpec(memory_space=pltpu.VMEM),
            scratch_shapes=[
                pltpu.VMEM((2, tokens, feats), jnp.bfloat16),
                pltpu.VMEM((n_pieces, d_model, PC), jnp.bfloat16),
                pltpu.VMEM((n_pieces, PC, feats), jnp.bfloat16),
                pltpu.VMEM((tokens, d_model), jnp.bfloat16),
                pltpu.VMEM((tokens, feats), jnp.float32),
                pltpu.VMEM((2, 1, feats), jnp.float32),
                pltpu.SemaphoreType.DMA((10,)),
                pltpu.SemaphoreType.DMA((4,)),
                pltpu.SemaphoreType.DMA((N_RECV,)),
            ],
            compiler_params=pltpu.CompilerParams(collective_id=0, has_side_effects=True, vmem_limit_bytes=52000000),
        )(*[pltpu.with_memory_space_constraint(a, pltpu.HBM) for a in ins])
        return y.reshape(x_blk.shape)

    return jax.shard_map(per_device, mesh=mesh, in_specs=(act_spec, P("col"), P("row", "col"), P("row", "col")), out_specs=act_spec, check_vma=False)
```

profile of v0, /device:TPU:0, one launch (start us, length us, event | category | flops | bytes accessed | tf_op | source)
XLA Modules:
  0.0 81.5 jit_solution(16404364984626188491)
XLA Ops:
  0.0 80.1 %mlp.1 = bf16[2048,512]{1,0:T(8,128)(2,1)S(1)} custom-call(bf16[2048,512]{1,0:T(8,128)(2,1)} %bitcast.4, f32[1,512]{1,0:T(1,128)} %bitcast.5, bf16[256,2048]{1,0:T(8,128)(2,1)} %w1_hbm.1, bf16[1024,512]{1,0:T(8,128)(2,1)} %w2_hbm.1), custom_call_target="tpu_custom_call" | custom-call | tf_op jit(solution)/shard_map/mlp/pallas_call | solution.py:281
  80.2 1.3 %copy.6 = bf16[2,1024,512]{2,1,0:T(8,128)(2,1)} copy(bf16[2,1024,512]{2,1,0:T(8,128)(2,1)S(1)} %bitcast.3) | data formatting | bytes 4194304
where the time goes:
time: 81.6 us; the launch traced here: 81.5 us
  Pallas kernels  80.1 us (98%)
  local copies, waits for them, and re-layouts  1.32 us (2%)
    pallas_call x1, Pallas kernels, per_device(): pl.pallas_call(kernel, name='mlp', out_shape=jax.ShapeDtypeStruct((tokens...  80.1 us

commit v1 on v0

--- a/solution.py
+++ b/solution.py
@@ -250,9 +250,11 @@
         layer_norm(4)
     with jax.named_scope("c_tiles"):
         last = pieces(col, 0, 8) + pieces(other, 0, 7)
-        unit(early, tokens - early, last[:8])
-        unit(early, tokens - early, last[8:])
-        finish()
+        for ps in (last[:8], last[8:]):
+            @pl.when(row >= 0)
+            def _():
+                unit(early, tokens - early, ps)
+                finish()
     b_arrived(7)
     with jax.named_scope("d_tile"):
         def write(rows, value):

time: 81.6 us -> 80.6 us (0.988)
  Pallas kernels: 80.1 us -> 79.2 us
    pallas_call x1, Pallas kernels: 80.1 us -> 79.2 us  [per_device(): pl.pallas_call(kernel, name='mlp', out_shape=jax.ShapeDtypeStruct((tokens...]
where the time goes in v1:
time: 80.6 us; the launch traced here: 80.5 us
  Pallas kernels  79.2 us (98%)
  local copies, waits for them, and re-layouts  1.32 us (2%)
    pallas_call x1, Pallas kernels, per_device(): pl.pallas_call(kernel, name='mlp', out_shape=jax.ShapeDtypeStruct((tokens...  79.2 us

profile of v1, /device:TPU:0, one launch (start us, length us, event | category | flops | bytes accessed | tf_op | source)
XLA Modules:
  0.0 80.5 jit_solution(17576463573892519863)
XLA Ops:
  0.0 79.2 %mlp.1 = bf16[2048,512]{1,0:T(8,128)(2,1)S(1)} custom-call(bf16[2048,512]{1,0:T(8,128)(2,1)} %bitcast.4, f32[1,512]{1,0:T(1,128)} %bitcast.5, bf16[256,2048]{1,0:T(8,128)(2,1)} %w1_hbm.1, bf16[1024,512]{1,0:T(8,128)(2,1)} %w2_hbm.1), custom_call_target="tpu_custom_call" | custom-call | tf_op jit(solution)/shard_map/mlp/pallas_call | solution.py:283
  79.2 1.3 %copy.6 = bf16[2,1024,512]{2,1,0:T(8,128)(2,1)} copy(bf16[2,1024,512]{2,1,0:T(8,128)(2,1)S(1)} %bitcast.3) | data formatting | bytes 4194304

commit v2 on v0

--- a/solution.py
+++ b/solution.py
@@ -250,16 +250,19 @@
         layer_norm(4)
     with jax.named_scope("c_tiles"):
         last = pieces(col, 0, 8) + pieces(other, 0, 7)
-        unit(early, tokens - early, last[:8])
-        unit(early, tokens - early, last[8:])
-        finish()
+        @pl.when(row >= 0)
+        def _():
+            unit(early, tokens - early, last)
+            finish()
     b_arrived(7)
     with jax.named_scope("d_tile"):
         def write(rows, value):
             ys[rows, :] = value.astype(jnp.bfloat16)
 
-        for q in range(4):
-            unit(q * (tokens // 4), tokens // 4, pieces(other, 7, 8), write)
+        r0 = 0
+        for n in (512, 512, 512, 384, 128):
+            unit(r0, n, pieces(other, 7, 8), write)
+            r0 += n
         finish()
 
     with jax.named_scope("sent"):

time: 81.6 us -> 80.8 us (level)
  no operation moved by 1% of the time
where the time goes in v2:
time: 80.8 us; the launch traced here: 80.7 us
  Pallas kernels  79.3 us (98%)
  local copies, waits for them, and re-layouts  1.32 us (2%)
    pallas_call x1, Pallas kernels, per_device(): pl.pallas_call(kernel, name='mlp', out_shape=jax.ShapeDtypeStruct((tokens...  79.3 us

profile of v2, /device:TPU:0, one launch (start us, length us, event | category | flops | bytes accessed | tf_op | source)
XLA Modules:
  0.0 80.7 jit_solution(11896883437223697387)
XLA Ops:
  0.0 79.3 %mlp.1 = bf16[2048,512]{1,0:T(8,128)(2,1)S(1)} custom-call(bf16[2048,512]{1,0:T(8,128)(2,1)} %bitcast.4, f32[1,512]{1,0:T(1,128)} %bitcast.5, bf16[256,2048]{1,0:T(8,128)(2,1)} %w1_hbm.1, bf16[1024,512]{1,0:T(8,128)(2,1)} %w2_hbm.1), custom_call_target="tpu_custom_call" | custom-call | tf_op jit(solution)/shard_map/mlp/pallas_call | solution.py:284
  79.3 1.3 %copy.6 = bf16[2,1024,512]{2,1,0:T(8,128)(2,1)} copy(bf16[2,1024,512]{2,1,0:T(8,128)(2,1)S(1)} %bitcast.3) | data formatting | bytes 4194304

commit v3 on v1

--- a/solution.py
+++ b/solution.py
@@ -11,8 +11,8 @@
 SQRT_2_OVER_PI = 0.7978845608028654
 X_ROWS = ((0, 512), (512, 512), (1024, 512), (1536, 320), (1856, 192))
 
-A_ICI, A_D2D, B_Y, B_X, B_D2D, X_Y, G_Y = 0, 4, 8, 24, 32, 40, 45
-N_RECV = 46
+A_ICI, A_D2D, B_Y, B_X, B_D2D, X_Y, G_Y = 0, 4, 8, 25, 33, 41, 46
+N_RECV = 47
 S_W1, S_W2, S_X, S_G = 0, 1, 2, 3
 
 
@@ -93,14 +93,19 @@
         send(w1p(col, 2 * s, row_x, 2), partner, S_W1, A_D2D + s)
         send(w2p(row_x, s), partner, S_W2, A_D2D + s)
 
-    def half_piece(half, e, h):
-        return w1s.at[half * 8 + e, pl.ds(pl.multiple_of(row * rows1 + h * (rows1 // 2), rows1 // 2), rows1 // 2)]
+    def part(half, e, h):
+        lo, n = ((0, 2), (2, 2))[h] if e != 6 else ((0, 2), (2, 1), (3, 1))[h]
+        q = rows1 // 4
+        return w1s.at[half * 8 + e, pl.ds(pl.multiple_of(row * rows1 + lo * q, q), n * q)]
+
+    def part_sem(e, h):
+        return B_Y + 2 * e + h + (e > 6)
 
     def relay_by(e, h):
-        part = half_piece(other, e, h)
-        wait(part, recv_sem.at[B_Y + 2 * e + h])
-        send(part, x_nbr, S_W1, B_X + e)
-        send(part, partner, S_W1, B_D2D + e)
+        rows = part(other, e, h)
+        wait(rows, recv_sem.at[part_sem(e, h)])
+        send(rows, x_nbr, S_W1, B_X + e)
+        send(rows, partner, S_W1, B_D2D + e)
 
     def relay_bx(e):
         wait(w1p(other, e, row_x), recv_sem.at[B_X + e])
@@ -160,8 +165,8 @@
                 issue(s + 2)
             if s == 1:
                 for e in range(8):
-                    for h in range(2):
-                        send(half_piece(col, e, h), y_nbr, S_W1, B_Y + 2 * e + h)
+                    for h in range(2 + (e == 6)):
+                        send(part(col, e, h), y_nbr, S_W1, part_sem(e, h))
                 send_x(4)
             relay_a(s)
         with jax.named_scope(f"a_norm{s}"):
@@ -226,13 +231,15 @@
     by(2, 0)
     a_unit(3)
     for e in range(5):
-        by(e + 2, 1)
+        by(e + 2, 1 + (e == 4))
         b_arrived(e)
         b_unit(e, 0)
         b_unit(e, 1)
         bx(e + 1)
         by(e + 3, 0)
         b_unit(e, 2)
+        if e == 3:
+            by(6, 1)
         b_unit(e, 3)
     by(7, 1)
     b_arrived(5)

time: 80.6 us -> 80.6 us (level)
  no operation moved by 1% of the time
where the time goes in v3:
time: 80.6 us; the launch traced here: 80.5 us
  Pallas kernels  79.2 us (98%)
  local copies, waits for them, and re-layouts  1.32 us (2%)
    pallas_call x1, Pallas kernels, per_device(): pl.pallas_call(kernel, name='mlp', out_shape=jax.ShapeDtypeStruct((tokens...  79.2 us

profile of v3, /device:TPU:0, one launch (start us, length us, event | category | flops | bytes accessed | tf_op | source)
XLA Modules:
  0.0 80.5 jit_solution(18070734036494795142)
XLA Ops:
  0.0 79.2 %mlp.1 = bf16[2048,512]{1,0:T(8,128)(2,1)S(1)} custom-call(bf16[2048,512]{1,0:T(8,128)(2,1)} %bitcast.4, f32[1,512]{1,0:T(1,128)} %bitcast.5, bf16[256,2048]{1,0:T(8,128)(2,1)} %w1_hbm.1, bf16[1024,512]{1,0:T(8,128)(2,1)} %w2_hbm.1), custom_call_target="tpu_custom_call" | custom-call | tf_op jit(solution)/shard_map/mlp/pallas_call | solution.py:290
  79.2 1.3 %copy.6 = bf16[2,1024,512]{2,1,0:T(8,128)(2,1)} copy(bf16[2,1024,512]{2,1,0:T(8,128)(2,1)S(1)} %bitcast.3) | data formatting | bytes 4194304

commit v4 on v1

--- a/solution.py
+++ b/solution.py
@@ -53,8 +53,8 @@
         for e in (2 * s, 2 * s + 1):
             cols = pl.ds((e % 2) * (4 * PC) + (e // 2) * PC, PC)
             dst = w1s.at[col * 8 + e, pl.ds(pl.multiple_of(row * rows1, rows1), rows1)]
-            pltpu.make_async_copy(w1_hbm.at[:, cols], dst, load_sem.at[s]).start()
-        pltpu.make_async_copy(w2_hbm.at[pl.ds(s * PC, PC)], w2p(row, s), load_sem.at[s]).start()
+            pltpu.make_async_copy(w1_hbm.at[:, cols], dst, load_sem.at[0 if s == 0 else 3]).start()
+        pltpu.make_async_copy(w2_hbm.at[pl.ds(s * PC, PC)], w2p(row, s), load_sem.at[0 if s == 0 else 3]).start()
 
     def x_part(h, i):
         r0, n = X_ROWS[i]
@@ -62,9 +62,9 @@
 
     def load_x(i):
         r0, n = X_ROWS[i]
-        pltpu.make_async_copy(x_hbm.at[pl.ds(r0, n)], x_part(col, i), load_sem.at[4 + i]).start()
-
-    pltpu.make_async_copy(g_hbm, gs.at[col], load_sem.at[9]).start()
+        pltpu.make_async_copy(x_hbm.at[pl.ds(r0, n)], x_part(col, i), load_sem.at[1 if i == 0 else 3]).start()
+
+    pltpu.make_async_copy(g_hbm, gs.at[col], load_sem.at[2]).start()
     for s in range(4):
         load_w(s)
         load_x(s)
@@ -76,11 +76,15 @@
     pl.semaphore_wait(barrier, 3)
 
     def send_x(i):
-        wait(x_part(col, i), load_sem.at[4 + i])
+        if i == 0:
+            wait(x_part(col, i), load_sem.at[1])
         send(x_part(col, i), y_nbr, S_X, X_Y + i)
 
     def issue(s):
-        wait(w1s.at[0], load_sem.at[s])
+        if s == 0:
+            wait(w1s.at[0], load_sem.at[0])
+        elif s == 1:
+            wait(w1s.at[pl.ds(0, 6)], load_sem.at[3])
         w1, w2 = w1p(col, 2 * s, row, 2), w2p(row, s)
         send(w1, x_nbr, S_W1, A_ICI + s)
         send(w2, x_nbr, S_W2, A_ICI + s)
@@ -149,7 +153,7 @@
         return [half * 8 + e for e in range(lo, hi)]
 
     with jax.named_scope("issue"):
-        wait(gs.at[col], load_sem.at[9])
+        wait(gs.at[col], load_sem.at[2])
         send(gs.at[col], y_nbr, S_G, G_Y)
         issue(0)
         issue(1)
@@ -293,7 +297,7 @@
                 pltpu.VMEM((tokens, d_model), jnp.bfloat16),
                 pltpu.VMEM((tokens, feats), jnp.float32),
                 pltpu.VMEM((2, 1, feats), jnp.float32),
-                pltpu.SemaphoreType.DMA((10,)),
+                pltpu.SemaphoreType.DMA((4,)),
                 pltpu.SemaphoreType.DMA((4,)),
                 pltpu.SemaphoreType.DMA((N_RECV,)),
             ],

time: 80.6 us -> 80.5 us (level)
  no operation moved by 1% of the time
where the time goes in v4:
time: 80.5 us; the launch traced here: 80.4 us
  Pallas kernels  79.1 us (98%)
  local copies, waits for them, and re-layouts  1.32 us (2%)
    pallas_call x1, Pallas kernels, per_device(): pl.pallas_call(kernel, name='mlp', out_shape=jax.ShapeDtypeStruct((tokens...  79.1 us

profile of v4, /device:TPU:0, one launch (start us, length us, event | category | flops | bytes accessed | tf_op | source)
XLA Modules:
  0.0 80.4 jit_solution(2276667661631931764)
XLA Ops:
  0.0 79.1 %mlp.1 = bf16[2048,512]{1,0:T(8,128)(2,1)S(1)} custom-call(bf16[2048,512]{1,0:T(8,128)(2,1)} %bitcast.4, f32[1,512]{1,0:T(1,128)} %bitcast.5, bf16[256,2048]{1,0:T(8,128)(2,1)} %w1_hbm.1, bf16[1024,512]{1,0:T(8,128)(2,1)} %w2_hbm.1), custom_call_target="tpu_custom_call" | custom-call | tf_op jit(solution)/shard_map/mlp/pallas_call | solution.py:287
  79.1 1.3 %copy.6 = bf16[2,1024,512]{2,1,0:T(8,128)(2,1)} copy(bf16[2,1024,512]{2,1,0:T(8,128)(2,1)S(1)} %bitcast.3) | data formatting | bytes 4194304
